TPU v7x, 256 devices: a whole 4x4x8 slice. The times are simulated.
256 devices in a mesh: node: 256 (over z, x, y, core).
Axes of the slice: x: 4, y: 4, z: 8, core: 2. Of those that a mesh axis runs over, the one named last changes fastest.
Arguments:
- round_index: int32 [1], replicated, may hold values from 0 to 63
- sample_ids: int32 [256, 8], P('node'), may hold values from 0 to 3
- token_pool: bfloat16 [256, 4, 64, 512], P('node'), may hold values from -20 to 20
- cotangent_pool: bfloat16 [256, 4, 64, 512], P('node'), may hold values from -6 to 6
- weights: bfloat16 [256, 4, 512, 512], P('node'), may hold values from -12 to 12
- residue: bfloat16 [256, 4, 512, 512], P('node'), may hold values from -6 to 6
Outputs:
- new_weights: bfloat16 [256, 4, 512, 512], P('node')
- new_residue: bfloat16 [256, 4, 512, 512], P('node')
- grad_rms: float32 [], replicated
All inputs are finite; a program needn't handle non-finite values.
Results may differ from a plain program's by a relative error of at most 0.0065.
Values may be sent and summed in bfloat16 or wider, within the bound.
A program may use at most 128 MiB of HBM per device.

v0:
```python
from functools import partial
import math

import jax
import jax.numpy as jnp
from jax import lax
from jax.sharding import Mesh
from jax.sharding import PartitionSpec as P

HEAD_DIM = 64
NODE = ("node_0", "node_1", "node_2", "node_3")


epsilon = 1e-06
step_rate = 0.1


def for_sending(x):

    def short(part):
        return part.astype(jnp.bfloat16) if part.dtype == jnp.float32 else part

    return jax.tree.map(short, x)


def from_behind(block, axis, distance):
    devices = range(lax.axis_size(axis))
    route = [((i - distance) % len(devices), i) for i in devices]
    return lax.ppermute(block, axis, route)


def one_axis_at_a_time(x, axes):
    for axis in axes:
        x = lax.psum(x, axis)
    return x


def normalize(tokens):
    values = tokens.astype(jnp.float32)
    centered = values - jnp.mean(values, -1, keepdims=True)
    variance = jnp.mean(centered * centered, -1, keepdims=True)
    return (centered * lax.rsqrt(variance + epsilon)).astype(jnp.bfloat16)


def attend(head_scale, block_data):
    queries, key_rows, value_rows, context_grad = block_data
    scores = (
        jnp.einsum("bshe,bthe->bhst", queries, key_rows, preferred_element_type=jnp.float32)
        * head_scale
    )
    attn_probs = jnp.exp(scores - jnp.max(scores, -1, keepdims=True))
    attn_probs = attn_probs / jnp.sum(attn_probs, -1, keepdims=True)
    probs_half = attn_probs.astype(jnp.bfloat16)
    context = jnp.einsum(
        "bhst,bthe->bshe", probs_half, value_rows, preferred_element_type=jnp.float32
    ).astype(jnp.bfloat16)
    probs_grad = jnp.einsum(
        "bshe,bthe->bhst", context_grad, value_rows, preferred_element_type=jnp.float32
    )
    value_grad = jnp.einsum(
        "bhst,bshe->bthe", probs_half, context_grad, preferred_element_type=jnp.float32
    ).astype(jnp.bfloat16)
    score_grad = (
        attn_probs * (probs_grad - jnp.sum(probs_grad * attn_probs, -1, keepdims=True)) * head_scale
    ).astype(jnp.bfloat16)
    query_grad = jnp.einsum(
        "bhst,bthe->bshe", score_grad, key_rows, preferred_element_type=jnp.float32
    ).astype(jnp.bfloat16)
    key_grad = jnp.einsum(
        "bhst,bshe->bthe", score_grad, queries, preferred_element_type=jnp.float32
    ).astype(jnp.bfloat16)
    return (context, query_grad, key_grad, value_grad)


def local_gradient(weights, tokens, cotangent):
    batch_size, seq_len, model_width = tokens.shape
    head_count = model_width // HEAD_DIM
    proj_scale = model_width ** (-0.5)
    row_count = batch_size * seq_len
    normed_rows = normalize(tokens).reshape(row_count, model_width)
    grad_rows = cotangent.reshape(row_count, model_width)
    projected = (
        jnp.einsum("td,mde->mte", normed_rows, weights[:3], preferred_element_type=jnp.float32)
        * proj_scale
    ).astype(jnp.bfloat16)
    context_grad = (
        jnp.einsum("te,de->td", grad_rows, weights[3], preferred_element_type=jnp.float32)
        * proj_scale
    ).astype(jnp.bfloat16)
    group_size = math.gcd(batch_size, max(1, 512 // seq_len))
    block_shape = (batch_size // group_size, group_size, seq_len, head_count, HEAD_DIM)
    blocks = (
        projected[0].reshape(block_shape),
        projected[1].reshape(block_shape),
        projected[2].reshape(block_shape),
        context_grad.reshape(block_shape),
    )
    context, query_grad, key_grad, value_grad = lax.map(partial(attend, HEAD_DIM ** (-0.5)), blocks)
    stacked = jnp.stack([query_grad, key_grad, value_grad]).reshape(3, row_count, model_width)
    input_grads = (
        jnp.einsum("td,mte->mde", normed_rows, stacked, preferred_element_type=jnp.float32)
        * proj_scale
    )
    output_grad = (
        jnp.einsum(
            "td,te->de",
            context.reshape(row_count, model_width),
            grad_rows,
            preferred_element_type=jnp.float32,
        )
        * proj_scale
    )
    return jnp.concatenate([input_grads, output_grad[None]], 0)


def tracked_from(payload, offset):
    return jax.tree.map(
        lambda part, own: part.astype(own.dtype),
        from_behind(for_sending(payload), NODE, offset),
        payload,
    )


def sent_from(payload, offset):
    return jax.tree.map(
        lambda part, own: part.astype(own.dtype),
        from_behind(for_sending(payload), NODE, offset),
        payload,
    )


def form_sent(weight_values, tracker):
    return (weight_values.astype(jnp.float32) - step_rate * tracker).astype(jnp.bfloat16)


def per_device(round_index, sample_ids, token_pool, cotangent_pool, weights, residue):
    node_count = lax.axis_size(NODE)
    levels = node_count.bit_length() - 1
    level_index = round_index[0] % levels
    own_weights = weights[0]
    sample_rows = sample_ids[0]
    tokens = jnp.take(token_pool[0], sample_rows, axis=0)
    cotangent = jnp.take(cotangent_pool[0], sample_rows, axis=0)
    gradient = local_gradient(own_weights, tokens, cotangent)
    total = one_axis_at_a_time(jnp.sum(gradient * gradient), NODE)
    tracked = (residue[0].astype(jnp.float32) + gradient).astype(jnp.bfloat16)
    near_sums = lax.switch(
        level_index,
        [partial(tracked_from, tracked, 2**shift_level) for shift_level in range(levels)],
    )
    tracker = 0.5 * (tracked.astype(jnp.float32) + near_sums.astype(jnp.float32))
    own_sent = form_sent(own_weights, tracker)
    peer_sent = lax.switch(
        level_index, [partial(sent_from, own_sent, 2**shift_level) for shift_level in range(levels)]
    )
    mixed = (
        0.5 * own_weights.astype(jnp.float32)
        + 0.5 * peer_sent.astype(jnp.float32)
        - 0.5 * step_rate * tracker
    )
    new_weights = mixed.astype(jnp.bfloat16)
    new_residue = (tracker - gradient).astype(jnp.bfloat16)
    grad_rms = jnp.sqrt(total / (node_count * gradient.size))
    return (new_weights[None], new_residue[None], grad_rms)


def solution(mesh):
    torus = Mesh(mesh.devices.reshape(8, 4, 4, 2), ("node_0", "node_1", "node_2", "node_3"))
    placed = (
        P(),
        P(NODE, None),
        P(NODE, None, None, None),
        P(NODE, None, None, None),
        P(NODE, None, None, None),
        P(NODE, None, None, None),
    )
    return jax.shard_map(
        per_device,
        mesh=torus,
        in_specs=placed,
        out_specs=(P(NODE, None, None, None), P(NODE, None, None, None), P()),
        check_vma=False,
    )
```

profile of v0, /device:TPU:1, one launch (start us, length us, event | category | flops | bytes accessed | tf_op | source)
XLA Modules:
  0.0 238.5 jit_solution(5347931693104690469)
XLA Ops:
  1.6 0.7 compare_and_fusion
  2.3 0.7 compare_select_fusion
  5.1 0.8 copy-done.10
  6.0 1.5 fusion.44
  8.0 0.8 copy.56
  8.8 2.4 %fusion.32 = bf16[3,512,512]{2,1,0:T(8,128)(2,1)S(1)} fusion(bf16[512,512,1]{1,0,2:T(8,128)(2,1)S(1)} %bitcast.78, bf16[1,4,512,512]{3,2,1,0:T(8,128)(2,1)} %param.28), kind=kOutput, calls=%fused_computation.39 | convolution fusion | flops 806879232 | bytes 3670016 | tf_op jit(solution)/shard_map/td,mde->mte/dot_general | solution.py:83
  11.2 1.1 fusion.64
  12.8 0.8 copy.50
  13.6 1.6 squeeze.42
  15.3 1.4 copy.62
  16.7 1.6 squeeze.38
  18.4 1.5 copy.53
  19.8 3.1 %fusion.66 = f32[8,8,64,64]{2,3,1,0:T(8,128)} fusion(bf16[8,64,8,64]{1,3,2,0:T(8,128)(2,1)S(1)} %copy.56, bf16[8,64,8,64]{1,3,2,0:T(8,128)(2,1)} %copy.62), kind=kOutput, calls=%fused_computation.78 | convolution fusion | flops 33554432 | bytes 2097152 | tf_op jit(solution)/shard_map/while/body/eval_jaxpr/bshe,bthe->bhst/dot_general | solution.py:57
  22.9 4.1 %copy.44 = bf16[1,4,512,512]{2,3,1,0:T(8,128)(2,1)} copy(bf16[1,4,512,512]{3,2,1,0:T(8,128)(2,1)} %param.28) | data formatting | bytes 4194304 | tf_op args[4]
  27.0 4.3 %copy.45 = bf16[1,4,512,512]{2,3,1,0:T(8,128)(2,1)} copy(bf16[1,4,512,512]{3,2,1,0:T(8,128)(2,1)} %param.29) | data formatting | bytes 4194304 | tf_op args[5]
  31.3 2.3 fusion.65
  33.5 2.3 fusion.35
  35.8 0.7 copy.92
  36.5 1.4 reshape.88
  38.0 5.4 %fusion.37 = bf16[8,64,8,64]{1,3,2,0:T(8,128)(2,1)} fusion(bf16[8,64,8,64]{1,3,2,0:T(8,128)(2,1)S(1)} %copy-done.9, f32[8,8,64,64]{2,3,1,0:T(8,128)} %fusion.66, f32[8,8,64,64]{2,3,1,0:T(8,128)} %get-tuple-element.90, f32[8,8,64]{2,1,0:T(8,128)S(1)} %get-tuple-element.89), kind=kOutput, calls=%fused_computation.42 | convolution fusion | flops 35655744 | bytes 3162112 | tf_op jit(solution)/shard_map/while/body/eval_jaxpr/bhst,bshe->bthe/dot_general | solution.py:69
  43.3 5.3 %fusion.40 = bf16[8,64,8,64]{1,3,2,0:T(8,128)(2,1)} fusion(bf16[8,64,8,64]{1,3,2,0:T(8,128)(2,1)S(1)} %copy.50, f32[8,8,64,64]{2,3,1,0:T(8,128)} %fusion.66, f32[8,8,64,64]{2,3,1,0:T(8,128)} %get-tuple-element.90, f32[8,8,64]{2,1,0:T(8,128)S(1)} %get-tuple-element.89), kind=kOutput, calls=%fused_computation.43 | convolution fusion | flops 35655744 | bytes 3162112 | tf_op jit(solution)/shard_map/while/body/eval_jaxpr/bhst,bthe->bshe/dot_general | solution.py:66
  48.6 2.0 fusion.36
  50.7 0.9 copy.64
  51.6 0.6 reshape.60
  53.1 2.0 copy.90
  55.1 1.4 reshape.86
  56.5 0.7 copy.91
  57.2 0.6 reshape.87
  57.8 2.5 %multiply_bitcast_fusion = f32[3,512,512]{1,2,0:T(8,128)S(1)} fusion(bf16[512,512,1]{1,0,2:T(8,128)(2,1)} %bitcast.79, bf16[1,512,512]{1,2,0:T(8,128)(2,1)} %reshape.88, bf16[1,512,512]{1,2,0:T(8,128)(2,1)S(1)} %reshape.87, bf16[1,512,512]{1,2,0:T(8,128)(2,1)} %reshape.86), kind=kOutput, calls=%fused_computation.16 | convolution fusion | flops 807665664 | bytes 5242880 | tf_op jit(solution)/shard_map/td,mte->mde/dot_general | solution.py:101
  60.3 1.6 copy-done.4
  61.9 0.8 fusion.6
  62.8 2.6 %copy.66 = bf16[4,512,512]{2,1,0:T(8,128)(2,1)} copy(bf16[4,512,512]{1,2,0:T(8,128)(2,1)S(1)} %fusion.6) | data formatting | bytes 4194304 | tf_op jit(solution)/shard_map/convert_element_type | solution.py:146
  65.4 54.2 %conditional.8 = (bf16[4,512,512]{2,1,0:T(8,128)(2,1)}) conditional(s32[]{:T(128)} %clamp.4, bf16[4,512,512]{2,1,0:T(8,128)(2,1)} %copy.66, bf16[4,512,512]{2,1,0:T(8,128)(2,1)} %copy.66, bf16[4,512,512]{2,1,0:T(8,128)(2,1)} %copy.66, bf16[4,512,512]{2,1,0:T(8,128)(2,1)} %copy.66, ...), branch_computations={%region_5.7_spmd, %region_6.8_spmd, %region_7.9_spmd, %region_8.10... | conditional | bytes 8388656
  65.4 2.0 collective-permute-start.3
  67.4 52.2 %collective-permute-done.3 = bf16[4,512,512]{2,1,0:T(8,128)(2,1)} collective-permute-done((bf16[4,512,512]{2,1,0:T(8,128)(2,1)}, bf16[4,512,512]{2,1,0:T(8,128)(2,1)}, u32[]{:S(2)}, u32[]{:S(2)}) %collective-permute-start.3) | collective-permute-done | bytes 2097184 | tf_op jit(solution)/shard_map/cond/branch_3_fun/ppermute | solution.py:29
  119.7 4.1 %copy.74 = bf16[4,512,512]{1,2,0:T(8,128)(2,1)} copy(bf16[4,512,512]{2,1,0:T(8,128)(2,1)} %get-tuple-element.91) | data formatting | bytes 4194304 | tf_op jit(solution)/shard_map/conditional.2
  123.8 3.7 %fusion.2 = bf16[4,512,512]{1,2,0:T(8,128)(2,1)S(1)} fusion(bf16[4,512,512]{1,2,0:T(8,128)(2,1)} %copy.74, bf16[4,512,512]{1,2,0:T(8,128)(2,1)} %copy-done.2, bf16[1,4,512,512]{2,3,1,0:T(8,128)(2,1)} %copy.44), kind=kLoop, calls=%fused_computation.6 | loop fusion | flops 7340032 | bytes 8388608 | tf_op jit(solution)/shard_map/convert_element_type | solution.py:133
  127.5 52.0 %conditional.9 = (bf16[4,512,512]{2,1,0:T(8,128)(2,1)}) conditional(s32[]{:T(128)} %clamp.4, bf16[4,512,512]{1,2,0:T(8,128)(2,1)S(1)} %fusion.2, bf16[4,512,512]{1,2,0:T(8,128)(2,1)S(1)} %fusion.2, bf16[4,512,512]{1,2,0:T(8,128)(2,1)S(1)} %fusion.2, bf16[4,512,512]{1,2,0:T(8,128)(2,1)S(1)} %fusion.2, ...), branch_computations={%region_13.15_spmd, %region_14.16_spmd, %region_15.17_spmd, %regio... | conditional | bytes 12582960
  127.6 2.4 %copy.78 = bf16[4,512,512]{2,1,0:T(8,128)(2,1)} copy(bf16[4,512,512]{1,2,0:T(8,128)(2,1)S(1)} %param.13) | data formatting | bytes 4194304 | tf_op jit(solution)/shard_map/convert_element_type
  130.0 49.6 %collective-permute-done.11 = bf16[4,512,512]{2,1,0:T(8,128)(2,1)} collective-permute-done((bf16[4,512,512]{2,1,0:T(8,128)(2,1)}, bf16[4,512,512]{2,1,0:T(8,128)(2,1)}, u32[]{:S(2)}, u32[]{:S(2)}) %collective-permute-start.11) | collective-permute-done | bytes 2097184 | tf_op jit(solution)/shard_map/cond/branch_3_fun/ppermute | solution.py:29
  179.6 4.3 %copy.83 = bf16[4,512,512]{1,2,0:T(8,128)(2,1)} copy(bf16[4,512,512]{2,1,0:T(8,128)(2,1)} %get-tuple-element.92) | data formatting | bytes 4194304 | tf_op jit(solution)/shard_map/conditional.3
  183.9 6.7 %multiply_reduce_fusion = (f32[]{:T(128)}, bf16[1,4,512,512]{2,3,1,0:T(8,128)(2,1)}, bf16[1,4,512,512]{2,3,1,0:T(8,128)(2,1)}) fusion(f32[1,512,512]{1,2,0:T(8,128)S(1)} %copy.65, f32[3,512,512]{1,2,0:T(8,128)} %copy-done.4, bf16[4,512,512]{1,2,0:T(8,128)(2,1)} %copy.74, bf16[4,512,512]{1,2,0:T(8,128)(2,1)S(1)} %copy-done.3, bf16[4,512,512]{1,2,0:T(8,128)(2,1)} %copy.83, ...), kind=kLoop, calls=%fused_computation.13 | loop fusion | flops 16777215 | bytes 16777220 | tf_op jit(solution)/shard_map/reduce_sum | solution.py:145
  190.6 11.3 %psum.28 = f32[]{:T(128)} all-reduce(f32[]{:T(128)} %get-tuple-element.83), channel_id=1, replica_groups=mesh['node_0'=8,'node_1'=4,'node_2'=4,'node_3'=2] {'node_0'}, use_global_device_ids=true, to_apply=%region_22.24 | all-reduce | flops 1 | bytes 8 | tf_op jit(solution)/shard_map/psum | solution.py:34
  201.8 6.6 %psum.29 = f32[]{:T(128)} all-reduce(f32[]{:T(128)} %psum.28), channel_id=1, replica_groups=mesh['node_0'=8,'node_1'=4,'node_2'=4,'node_3'=2] {'node_1'}, use_global_device_ids=true, to_apply=%region_23.25 | all-reduce | flops 1 | bytes 8 | tf_op jit(solution)/shard_map/psum | solution.py:34
  208.5 9.3 %psum.30 = f32[]{:T(128)} all-reduce(f32[]{:T(128)} %psum.29), channel_id=1, replica_groups=mesh['node_0'=8,'node_1'=4,'node_2'=4,'node_3'=2] {'node_2'}, use_global_device_ids=true, to_apply=%region_24.26 | all-reduce | flops 1 | bytes 8 | tf_op jit(solution)/shard_map/psum | solution.py:34
  217.8 12.2 %psum.31 = f32[]{:T(128)} all-reduce(f32[]{:T(128)} %psum.30), channel_id=1, replica_groups=mesh['node_0'=8,'node_1'=4,'node_2'=4,'node_3'=2] {'node_3'}, use_global_device_ids=true, to_apply=%region_25.27 | all-reduce | flops 1 | bytes 8 | tf_op jit(solution)/shard_map/psum | solution.py:34
  230.7 4.3 %copy.85 = bf16[1,4,512,512]{3,2,1,0:T(8,128)(2,1)} copy(bf16[1,4,512,512]{2,3,1,0:T(8,128)(2,1)} %get-tuple-element.84) | data formatting | bytes 4194304
  235.0 2.4 copy.84
  (42 shorter events, 4.3 us)
Async XLA Ops:
  0.6 1.0 copy-start
  0.6 3.8 %copy-start.13 = (bf16[1,4,64,512]{3,2,1,0:T(8,128)(2,1)S(1)}, bf16[1,4,64,512]{3,2,1,0:T(8,128)(2,1)}, u32[]{:S(2)}) copy-start(bf16[1,4,64,512]{3,2,1,0:T(8,128)(2,1)} %param.27) | copy-start | bytes 786436
  4.4 4.4 %copy-start.14 = (bf16[8,64,512]{2,1,0:T(8,128)(2,1)}, bf16[8,64,512]{2,1,0:T(8,128)(2,1)S(1)}, u32[]{:S(2)}) copy-start(bf16[8,64,512]{2,1,0:T(8,128)(2,1)S(1)} %fusion.48) | copy-start | bytes 1572868
  5.1 0.8 copy-start.10
  27.0 4.3 %copy-start.8 = (bf16[8,64,8,64]{1,3,2,0:T(8,128)(2,1)S(1)}, bf16[8,64,8,64]{1,3,2,0:T(8,128)(2,1)}, u32[]{:S(2)}) copy-start(bf16[8,64,8,64]{1,3,2,0:T(8,128)(2,1)} %copy.53) | copy-start | bytes 1572868
  35.8 2.2 copy-start.9
  43.3 5.3 %copy-start.7 = (bf16[8,64,8,64]{1,3,2,0:T(8,128)(2,1)S(1)}, bf16[8,64,8,64]{1,3,2,0:T(8,128)(2,1)}, u32[]{:S(2)}) copy-start(bf16[8,64,8,64]{1,3,2,0:T(8,128)(2,1)} %copy.62) | copy-start | bytes 1572868
  50.7 1.6 copy-start.11
  53.1 3.4 %copy-start.12 = (bf16[8,64,8,64]{1,3,2,0:T(8,128)(2,1)S(1)}, bf16[8,64,8,64]{1,3,2,0:T(8,128)(2,1)}, u32[]{:S(2)}) copy-start(bf16[8,64,8,64]{1,3,2,0:T(8,128)(2,1)} %fusion.37) | copy-start | bytes 1572868
  57.8 4.2 %copy-start.6 = (bf16[1,4,512,512]{2,3,1,0:T(8,128)(2,1)S(1)}, bf16[1,4,512,512]{2,3,1,0:T(8,128)(2,1)}, u32[]{:S(2)}) copy-start(bf16[1,4,512,512]{2,3,1,0:T(8,128)(2,1)} %copy.45) | copy-start | bytes 6291460
  60.3 1.6 copy-start.4
  62.8 2.7 %copy-start.2 = (bf16[4,512,512]{1,2,0:T(8,128)(2,1)}, bf16[4,512,512]{1,2,0:T(8,128)(2,1)S(1)}, u32[]{:S(2)}) copy-start(bf16[4,512,512]{1,2,0:T(8,128)(2,1)S(1)} %fusion.6) | copy-start | bytes 6291460
  65.4 54.2 %collective-permute-start.3 = (bf16[4,512,512]{2,1,0:T(8,128)(2,1)}, bf16[4,512,512]{2,1,0:T(8,128)(2,1)}, u32[]{:S(2)}, u32[]{:S(2)}) collective-permute-start(bf16[4,512,512]{2,1,0:T(8,128)(2,1)} %param.5), channel_id=1, source_target_pairs={{248,0},{249,1},{250,2},{251,3},{252,4},{253,5},{254,6},{255,7},{0... | collective-permute-start | bytes 6291464 | tf_op jit(solution)/shard_map/cond/branch_3_fun/ppermute | solution.py:29
  130.0 49.6 %collective-permute-start.11 = (bf16[4,512,512]{2,1,0:T(8,128)(2,1)}, bf16[4,512,512]{2,1,0:T(8,128)(2,1)}, u32[]{:S(2)}, u32[]{:S(2)}) collective-permute-start(bf16[4,512,512]{2,1,0:T(8,128)(2,1)} %copy.78), channel_id=1, source_target_pairs={{248,0},{249,1},{250,2},{251,3},{252,4},{253,5},{254,6},{255,7},{0... | collective-permute-start | bytes 6291464 | tf_op jit(solution)/shard_map/cond/branch_3_fun/ppermute | solution.py:29
  179.6 4.3 %copy-start.3 = (bf16[4,512,512]{1,2,0:T(8,128)(2,1)S(1)}, bf16[4,512,512]{1,2,0:T(8,128)(2,1)}, u32[]{:S(2)}) copy-start(bf16[4,512,512]{1,2,0:T(8,128)(2,1)} %copy-done.2) | copy-start | bytes 6291460
  230.7 4.3 %copy-start.5 = (bf16[1,4,512,512]{2,3,1,0:T(8,128)(2,1)S(1)}, bf16[1,4,512,512]{2,3,1,0:T(8,128)(2,1)}, u32[]{:S(2)}) copy-start(bf16[1,4,512,512]{2,3,1,0:T(8,128)(2,1)} %get-tuple-element.85) | copy-start | bytes 6291460
  230.7 6.7 %copy-start.1 = (bf16[1,4,64,512]{3,2,1,0:T(8,128)(2,1)S(1)}, bf16[1,4,64,512]{3,2,1,0:T(8,128)(2,1)}, u32[]{:S(2)}) copy-start(bf16[1,4,64,512]{3,2,1,0:T(8,128)(2,1)} %param.26) | copy-start | bytes 786436
where the time goes:
time: 239 us
  waiting for transfers between devices  102 us (43%)
  local copies, waits for them, and re-layouts  51.1 us (21%)
  blocking collectives  39.5 us (17%)
  matrix products  27.1 us (11%)
  other arithmetic  13.5 us (6%)
  between operations  3.5 us (1%)
    ppermute x2, waiting for transfers between devices, from_behind(): return lax.ppermute(block, axis, route)  102 us
    psum x4, blocking collectives, one_axis_at_a_time(): x = lax.psum(x, axis)  39.5 us
    unnamed x34, local copies, waits for them, and re-layouts  17.8 us
    squeeze x8, local copies, waits for them, and re-layouts, local_gradient(): lax.map(partial(attend, HEAD_DIM ** (-0.5)), blocks)  8.82 us
    another operation x2, local copies, waits for them, and re-layouts  8.45 us
    another operation x6, local copies, waits for them, and re-layouts, local_gradient(): jnp.stack([query_grad, key_grad, value_grad])  6.85 us
    reduce_sum x1, other arithmetic, per_device(): total = one_axis_at_a_time(jnp.sum(gradient * gradient), NODE)  6.66 us
    dot_general x1, matrix products, attend(): jnp.einsum('bhst,bshe->bthe', score_grad, queries, preferred_element_type...  5.36 us
  transfers between devices with their start and end apart: 2, of which 2 were waited for; matrix products, arithmetic and copies ran while one was open for 0% of the time, Pallas kernels for 0%

commit v1 on v0

v1 whole, which is shorter than its diff:
```python
from functools import partial

import jax
import jax.numpy as jnp
from jax import lax
from jax.experimental import pallas as pl
from jax.experimental.pallas import tpu as pltpu
from jax.sharding import PartitionSpec as P

HEAD_DIM = 64
EPSILON = 1e-06
STEP_RATE = 0.1
ROWS = 128
WINDOW = 4

F32, BF16 = jnp.float32, jnp.bfloat16
VMEM, SMEM, ANY = pltpu.VMEM, pltpu.SMEM, pl.ANY


def dot(a, b, contract):
    return lax.dot_general(a, b, ((contract[:1], contract[1:]), ((), ())), preferred_element_type=F32)


def local_kernel(ids_ref, token_ref, cot_ref, w_ref, left_ref, right_ref, q_s, k_s, v_s, c_s):
    pool, seq, width = token_ref.shape
    rows = pool * seq
    proj_scale = width**-0.5
    head_scale = HEAD_DIM**-0.5
    counts = []
    for image in range(pool):
        n = jnp.int32(0)
        for b in range(ids_ref.shape[1]):
            n = n + (ids_ref[0, b] == image).astype(jnp.int32)
        counts.append(n.astype(F32))

    x = token_ref[...].reshape(rows, width).astype(F32)
    centered = x - jnp.mean(x, -1, keepdims=True)
    variance = jnp.mean(centered * centered, -1, keepdims=True)
    normed = (centered * lax.rsqrt(variance + EPSILON)).astype(BF16)
    left_ref[0] = normed.T
    for which, out in enumerate((q_s, k_s, v_s)):
        out[...] = (dot(normed, w_ref[which], (1, 0)) * proj_scale).astype(BF16)
    cot = cot_ref[...].reshape(rows, width)
    right_ref[3] = cot
    cg = dot(cot, w_ref[3], (1, 1))
    for image in range(pool):
        at = slice(image * seq, (image + 1) * seq)
        c_s[at] = (cg[at] * (proj_scale * counts[image])).astype(BF16)

    pair = 2 * seq
    lane = lax.broadcasted_iota(jnp.int32, (pair, 128), 1) < HEAD_DIM
    near = lax.broadcasted_iota(jnp.int32, (seq, 128), 1) < seq
    zero = jnp.zeros((pair, 128), BF16)
    zero_half = jnp.zeros((seq, 128), BF16)

    def by_head(block):
        return jnp.concatenate([jnp.where(lane, block, zero), jnp.where(lane, zero, block)], 0)

    def packed(block):
        return jnp.where(near, block[:seq], block[seq:])

    def spread(block):
        return jnp.concatenate([jnp.where(near, block, zero_half), jnp.where(near, zero_half, block)], 0)

    for b in range(pool // 2):
        at = slice(b * pair, (b + 1) * pair)
        count = jnp.where(near[:1], counts[2 * b], counts[2 * b + 1])
        for j in range(width // 128):
            cols = slice(j * 128, (j + 1) * 128)
            q, k, v, c = q_s[at, cols], k_s[at, cols], v_s[at, cols], c_s[at, cols]
            kk, vv = by_head(k), by_head(v)
            scores = dot(kk, q, (1, 1)) * head_scale
            grads = dot(vv, c, (1, 1))
            probs, back = [], []
            for h in range(2):
                of_head = slice(h * pair, (h + 1) * pair)
                s = packed(scores[of_head])
                e = jnp.exp(s - jnp.max(s, 0, keepdims=True))
                p = e * (1.0 / jnp.sum(e, 0, keepdims=True))
                g = packed(grads[of_head])
                d = p * (g - jnp.sum(g * p, 0, keepdims=True)) * head_scale
                probs.append(spread(p.astype(BF16)))
                back.append(spread(d.astype(BF16)))
            p_rows, d_rows = jnp.concatenate(probs, 0), jnp.concatenate(back, 0)
            p_cols, d_cols = jnp.concatenate(probs, 1), jnp.concatenate(back, 1)
            left_ref[1, cols, at] = (dot(vv, p_rows, (0, 0)) * count).astype(BF16)
            right_ref[0, at, cols] = dot(d_rows, kk, (0, 0)).astype(BF16)
            right_ref[1, at, cols] = dot(d_cols, by_head(q), (1, 0)).astype(BF16)
            right_ref[2, at, cols] = dot(p_cols, by_head(c), (1, 0)).astype(BF16)


def local_part(sample_ids, tokens, cotangent, weights):
    pool, seq, width = tokens.shape
    rows = pool * seq
    return pl.pallas_call(
        local_kernel,
        out_shape=(
            jax.ShapeDtypeStruct((2, width, rows), BF16),
            jax.ShapeDtypeStruct((4, rows, width), BF16),
        ),
        in_specs=[pl.BlockSpec(memory_space=SMEM)] + [pl.BlockSpec(memory_space=VMEM)] * 3,
        out_specs=(pl.BlockSpec(memory_space=VMEM), pl.BlockSpec(memory_space=VMEM)),
        scratch_shapes=[VMEM((rows, width), BF16)] * 4,
        compiler_params=pltpu.CompilerParams(vmem_limit_bytes=32 << 20),
        cost_estimate=pl.CostEstimate(flops=2 * 4 * rows * width * width, bytes_accessed=4 << 20, transcendentals=rows * width),
        name="local",
    )(sample_ids, tokens, cotangent, weights)


def exchange_kernel(
    sizes,
    distance,
    left_ref,
    right_ref,
    w_hbm,
    r_hbm,
    new_w_hbm,
    new_r_hbm,
    rms_ref,
    w_v,
    r_v,
    grad,
    mine,
    sent,
    got_t,
    got_s,
    out_w,
    out_r,
    square,
    parts,
    w_sem,
    r_sem,
    send_sem,
    recv_sem,
    ow_sem,
    or_sem,
    part_send,
    part_recv,
):
    total = 1
    for size in sizes:
        total *= size
    width = w_hbm.shape[-1]
    per = width // ROWS
    chunks = 4 * per
    proj_scale = width**-0.5
    mutual = (2 * distance) % total == 0
    me = lax.axis_index("node")
    ahead = lax.rem(me + distance, total)
    behind = lax.rem(me + total - distance, total)

    groups = []
    stride = 1
    first = 0
    for size in reversed(sizes):
        place = lax.rem(me // stride, size)
        base = me - place * stride
        others = [base + lax.rem(place + d, size) * stride for d in range(1, size)]
        places = [lax.rem(place + d, size) for d in range(1, size)]
        groups.append((first, size, place, others, places))
        first += size
        stride *= size

    barrier = pltpu.get_barrier_semaphore()
    count = 1
    pl.semaphore_signal(barrier, inc=1, device_id=(behind,), device_id_type=pl.DeviceIdType.MESH)
    for _, size, _, others, _ in groups:
        for other in others:
            pl.semaphore_signal(barrier, inc=1, device_id=(other,), device_id_type=pl.DeviceIdType.MESH)
            count += 1

    def at(chunk):
        return chunk // per, pl.ds(pl.multiple_of(lax.rem(chunk, per) * ROWS, ROWS), ROWS)

    def load_r(chunk):
        m, rows = at(chunk)
        return pltpu.make_async_copy(r_hbm.at[m, rows], r_v.at[m, rows], r_sem.at[chunk])

    def load_w(m):
        return pltpu.make_async_copy(w_hbm.at[m], w_v.at[m], w_sem.at[m])

    for chunk in range(chunks):
        load_r(jnp.int32(chunk)).start()
    for m in range(4):
        load_w(m).start()

    square[...] = jnp.zeros_like(square)

    def compute(chunk):
        m, rows = at(chunk)
        g = dot(left_ref[m // 3, rows, :], right_ref[m], (1, 0)) * proj_scale
        load_r(chunk).wait()
        grad[m, rows, :] = g
        mine[m, rows, :] = (r_v[m, rows, :].astype(F32) + g).astype(BF16)
        square[...] += jnp.sum((g * g).reshape(ROWS // 8, 8, width), 0)

    def send(item):
        chunk = lax.rem(item, chunks)
        m, rows = at(chunk)

        def copy(source, target):
            return pltpu.make_async_remote_copy(
                src_ref=source.at[m, rows],
                dst_ref=target.at[m, rows],
                send_sem=send_sem.at[item],
                recv_sem=recv_sem.at[item],
                device_id=(ahead,),
                device_id_type=pl.DeviceIdType.MESH,
            )

        return copy

    early, late = ((w_v, got_s), (mine, got_t)) if mutual else ((mine, got_t), (sent, got_s))

    def write_r(chunk):
        m, rows = at(chunk)
        return pltpu.make_async_copy(out_r.at[m, rows], new_r_hbm.at[m, rows], or_sem.at[chunk])

    def write_w(chunk):
        m, rows = at(chunk)
        return pltpu.make_async_copy(out_w.at[m, rows], new_w_hbm.at[m, rows], ow_sem.at[chunk])

    def on_tracked(chunk):
        m, rows = at(chunk)
        tracker = 0.5 * (mine[m, rows, :].astype(F32) + got_t[m, rows, :].astype(F32))
        w = w_v[m, rows, :].astype(F32)
        if mutual:
            theirs = (got_s[m, rows, :].astype(F32) - STEP_RATE * tracker).astype(BF16).astype(F32)
            out_w[m, rows, :] = (0.5 * w + 0.5 * theirs - 0.5 * STEP_RATE * tracker).astype(BF16)
        else:
            sent[m, rows, :] = (w - STEP_RATE * tracker).astype(BF16)
        out_r[m, rows, :] = (tracker - grad[m, rows, :]).astype(BF16)
        write_r(chunk).start()
        if mutual:
            write_w(chunk).start()

    def on_sent(chunk):
        m, rows = at(chunk)
        tracker = 0.5 * (mine[m, rows, :].astype(F32) + got_t[m, rows, :].astype(F32))
        w = w_v[m, rows, :].astype(F32)
        out_w[m, rows, :] = (0.5 * w + 0.5 * got_s[m, rows, :].astype(F32) - 0.5 * STEP_RATE * tracker).astype(BF16)
        write_w(chunk).start()

    def part_copy(k, d):
        start, size, place, others, places = groups[k]
        return pltpu.make_async_remote_copy(
            src_ref=parts.at[start + place],
            dst_ref=parts.at[start + place],
            send_sem=part_send.at[start + d],
            recv_sem=part_recv.at[start + place],
            device_id=(others[d],),
            device_id_type=pl.DeviceIdType.MESH,
        )

    def part_arrival(k, d):
        start, size, place, others, places = groups[k]
        return pltpu.make_async_remote_copy(
            src_ref=parts.at[start + places[d]],
            dst_ref=parts.at[start + places[d]],
            send_sem=part_send.at[start + d],
            recv_sem=part_recv.at[start + places[d]],
            device_id=(others[d],),
            device_id_type=pl.DeviceIdType.MESH,
        )

    def fold(k):
        start, size = groups[k][:2]
        value = parts[start]
        for n in range(1, size):
            value = value + parts[start + n]
        return value

    active = [k for k in range(len(groups)) if groups[k][1] > 1]

    def put_part(k, value):
        parts[groups[k][0] + groups[k][2]] = value

    def start_part(k):
        for d in range(groups[k][1] - 1):
            part_copy(k, d).start()

    def end_part(k):
        for d in range(groups[k][1] - 1):
            part_arrival(k, d).wait_recv()
        for d in range(groups[k][1] - 1):
            part_copy(k, d).wait_send()

    if mutual:
        for m in range(4):
            load_w(m).wait()
    else:
        compute(jnp.int32(0))
    pl.semaphore_wait(barrier, count)
    skip = 0 if mutual else 1
    first_part = chunks // 2 + 1

    def step(n, carry):
        @pl.when(n < 2 * chunks)
        def _():
            @pl.when(n >= WINDOW)
            def _():
                send(n - WINDOW)(*early).wait_send()

            @pl.when(n < chunks)
            def _():
                send(n)(*early).start()

            @pl.when(n >= chunks)
            def _():
                send(n)(*late).start()

        for extra in range(2):
            chunk = 2 * n + extra + skip

            @pl.when(chunk < chunks)
            def _():
                compute(chunk)

        for order, k in enumerate(active):

            @pl.when(n == first_part + 3 * order)
            def _():
                if order == 0:
                    value = square[:, :128]
                    for lanes in range(1, width // 128):
                        value = value + square[:, lanes * 128 : (lanes + 1) * 128]
                else:
                    end_part(active[order - 1])
                    value = fold(active[order - 1])
                put_part(k, value)

            @pl.when(n == first_part + 3 * order + 1)
            def _():
                start_part(k)

        got = n - WINDOW

        @pl.when(jnp.logical_and(got >= 0, got < chunks))
        def _():
            if not mutual:
                @pl.when(got == 0)
                def _():
                    for m in range(4):
                        load_w(m).wait()

            send(got)(*early).wait_recv()
            if not mutual:
                on_tracked(got)

        @pl.when(got >= chunks)
        def _():
            send(got)(*late).wait_recv()
            if mutual:
                on_tracked(got - chunks)
            else:
                on_sent(got - chunks)

        return carry

    lax.fori_loop(0, 2 * chunks + WINDOW, step, 0)
    end_part(active[-1])
    value = fold(active[-1])
    mean = jnp.sum(jnp.sum(value, 1, keepdims=True), 0, keepdims=True) / (total * 4 * width * width)
    rms_ref[0] = jnp.sqrt(jnp.broadcast_to(mean, (8, 128)))[0, 0]

    def drain(n, carry):
        write_r(n).wait()
        write_w(n).wait()
        return carry

    def settle(n, carry):
        send(n)(*late).wait_send()
        return carry

    lax.fori_loop(2 * chunks - WINDOW, 2 * chunks, settle, 0)
    lax.fori_loop(0, chunks, drain, 0)


def exchange_part(sizes, level, left, right, weights, residue):
    shape = weights.shape
    whole = (shape, BF16)
    chunks = 4 * (shape[-1] // ROWS)
    places = sum(sizes)
    dma = pltpu.SemaphoreType.DMA
    return pl.pallas_call(
        partial(exchange_kernel, sizes, 2**level),
        out_shape=(
            jax.ShapeDtypeStruct(shape, BF16),
            jax.ShapeDtypeStruct(shape, BF16),
            jax.ShapeDtypeStruct((1,), F32),
        ),
        in_specs=[pl.BlockSpec(memory_space=VMEM)] * 2 + [pl.BlockSpec(memory_space=ANY)] * 2,
        out_specs=(pl.BlockSpec(memory_space=ANY), pl.BlockSpec(memory_space=ANY), pl.BlockSpec(memory_space=SMEM)),
        scratch_shapes=[
            VMEM(*whole),
            VMEM(*whole),
            VMEM(shape, F32),
            VMEM(*whole),
            VMEM(*whole),
            VMEM(*whole),
            VMEM(*whole),
            VMEM(*whole),
            VMEM(*whole),
            VMEM((8, shape[-1]), F32),
            VMEM((places, 8, 128), F32),
            dma((4,)),
            dma((chunks,)),
            dma((2 * chunks,)),
            dma((2 * chunks,)),
            dma((chunks,)),
            dma((chunks,)),
            dma((places,)),
            dma((places,)),
        ],
        compiler_params=pltpu.CompilerParams(
            collective_id=level, has_side_effects=True, vmem_limit_bytes=40 << 20
        ),
        name=f"exchange_{level}",
    )(left, right, weights, residue)


def per_device(sizes, levels, round_index, sample_ids, token_pool, cotangent_pool, weights, residue):
    left, right = local_part(sample_ids, token_pool[0], cotangent_pool[0], weights[0])
    new_weights, new_residue, rms = lax.switch(
        round_index[0] % levels,
        [partial(exchange_part, sizes, level) for level in range(levels)],
        left,
        right,
        weights[0],
        residue[0],
    )
    return new_weights[None], new_residue[None], rms.reshape(())


def solution(mesh):
    nodes = mesh.shape["node"]
    sizes = {256: (8, 4, 4, 2), 16: (2, 2, 2, 2), 8: (2, 1, 2, 2), 4: (1, 1, 2, 2)}[nodes]
    levels = nodes.bit_length() - 1
    split = (P(), P("node", None)) + (P("node", None, None, None),) * 4
    return jax.shard_map(
        partial(per_device, sizes, levels),
        mesh=mesh,
        in_specs=split,
        out_specs=(P("node", None, None, None), P("node", None, None, None), P()),
        check_vma=False,
    )
```

time: 239 us -> 118 us (0.49)
  Pallas kernels: 0 us -> 110 us
  waiting for transfers between devices: 102 us -> 0 us
  local copies, waits for them, and re-layouts: 51.1 us -> 5.19 us
  blocking collectives: 39.5 us -> 0 us
  matrix products: 27.1 us -> 0 us
  other arithmetic: 13.5 us -> 0 us
    pallas_call x0 -> x2, Pallas kernels: none -> 110 us  [the longest x1 105 us: exchange_part(): pl.pallas_call(partial(exchange_kernel, sizes, 2 ** level), out_shape=(ja...]
    ppermute x2 -> x0, waiting for transfers between devices: 102 us -> none  [from_behind(): return lax.ppermute(block, axis, route)]
    psum x4 -> x0, blocking collectives: 39.5 us -> none  [one_axis_at_a_time(): x = lax.psum(x, axis)]
    dot_general x9 -> x0, matrix products: 24.9 us -> none  [the longest x1 5.36 us: attend(): jnp.einsum('bhst,bshe->bthe', score_grad, queries, preferred_element_type...]
    another operation x8 -> x0, local copies, waits for them, and re-layouts: 15.3 us -> none
    unnamed x34 -> x10, local copies, waits for them, and re-layouts: 17.8 us -> 5.19 us
    squeeze x8 -> x0, local copies, waits for them, and re-layouts: 8.82 us -> none  [local_gradient(): lax.map(partial(attend, HEAD_DIM ** (-0.5)), blocks)]
    reduce_sum x3 -> x0, other arithmetic: 7.25 us -> none  [the longest x1 6.66 us: per_device(): total = one_axis_at_a_time(jnp.sum(gradient * gradient), NODE)]
  transfers between devices with their start and end apart: 2 -> 0, of which waited for: 2 -> 0; matrix products, arithmetic and copies ran while one was open for 0% -> 0% of each run, Pallas kernels for 0% -> 0%
where the time goes in v1:
time: 118 us; the launch traced here: 119 us
  Pallas kernels  110 us (93%)
  local copies, waits for them, and re-layouts  5.19 us (4%)
  between operations  3.09 us (3%)
    pallas_call x1, Pallas kernels, exchange_part(): pl.pallas_call(partial(exchange_kernel, sizes, 2 ** level), out_shape=(ja...  105 us
    unnamed x10, local copies, waits for them, and re-layouts  5.19 us
    pallas_call x1, Pallas kernels, local_part(): pl.pallas_call(local_kernel, out_shape=(jax.ShapeDtypeStruct((2, width, r...  5.1 us

profile of v1, /device:TPU:1, one launch (start us, length us, event | category | flops | bytes accessed | tf_op | source)
XLA Modules:
  0.0 118.7 jit_solution(15800646038115167438)
XLA Ops:
  1.3 0.0 copy-start
  1.3 0.9 copy-done
  2.2 0.0 copy-start.1
  2.2 0.9 copy-done.1
  3.2 0.0 copy-start.2
  3.2 0.7 copy-done.2
  3.9 0.0 copy-start.3
  3.9 5.1 %local.1 = (bf16[2,512,256]{2,1,0:T(8,128)(2,1)S(1)}, bf16[4,256,512]{2,1,0:T(8,128)(2,1)S(1)}) custom-call(s32[1,8]{1,0:T(1,128)S(1)} %copy-done.2, bf16[4,64,512]{2,1,0:T(8,128)(2,1)S(1)} %bitcast.18, bf16[4,64,512]{2,1,0:T(8,128)(2,1)S(1)} %bitcast.19, bf16[4,512,512]{2,1,0:T(8,128)(2,1)} %bitcast.20), custom_call_target="tpu_custom_call" | custom-call | flops 536870912 | bytes 4194304 | tf_op jit(solution)/shard_map/local/pallas_call | solution.py:95
  9.0 0.0 copy-done.3
  9.0 105.3 %conditional.1 = ((bf16[4,512,512]{2,1,0:T(8,128)(2,1)S(1)}, bf16[4,512,512]{2,1,0:T(8,128)(2,1)S(1)}, f32[1]{0:T(128)})) conditional(s32[]{:T(128)} %clamp.3, (bf16[1,4,512,512]{3,2,1,0:T(8,128)(2,1)}, bf16[2,512,256]{2,1,0:T(8,128)(2,1)S(1)}, bf16[4,256,512]{2,1,0:T(8,128)(2,1)S(1)}, ...), branch_computations={%region_0.1_spmd, %region_1.2_spmd, %region_2.3_spmd, %region_3.4_... | conditional | bytes 8 | solution.py:424
  9.0 105.0 %exchange_3.1 = (bf16[4,512,512]{2,1,0:T(8,128)(2,1)S(1)}, bf16[4,512,512]{2,1,0:T(8,128)(2,1)S(1)}, f32[1]{0:T(128)}) custom-call(bf16[2,512,256]{2,1,0:T(8,128)(2,1)S(1)} %get-tuple-element.120.left_ref, bf16[4,256,512]{2,1,0:T(8,128)(2,1)S(1)} %get-tuple-element.121.right_ref, bf16[4,512,512]{2,1,0:T(8,128)(2,1)S(1)} %get-tuple-element.122.w_hbm, ...), custom_call_target="tpu_custom_call" | custom-call | tf_op jit(solution)/shard_map/cond/branch_3_fun/exchange_3/pallas_call | solution.py:385
  114.3 1.3 %copy.37 = bf16[1,4,512,512]{3,2,1,0:T(8,128)(2,1)} copy(bf16[1,4,512,512]{3,2,1,0:T(8,128)(2,1)S(1)} %bitcast.37) | data formatting | bytes 4194304
  115.6 1.3 %copy.38 = bf16[1,4,512,512]{3,2,1,0:T(8,128)(2,1)} copy(bf16[1,4,512,512]{3,2,1,0:T(8,128)(2,1)S(1)} %bitcast.38) | data formatting | bytes 4194304
Async XLA Ops:
  1.3 1.0 copy-start
  2.2 0.9 copy-start.1
  3.2 0.7 copy-start.2
  3.9 5.1 %copy-start.3 = (bf16[1,4,512,512]{3,2,1,0:T(8,128)(2,1)S(1)}, bf16[1,4,512,512]{3,2,1,0:T(8,128)(2,1)}, u32[]{:S(2)}) copy-start(bf16[1,4,512,512]{3,2,1,0:T(8,128)(2,1)} %param.18) | copy-start | bytes 6291460
